TPU v7x, 768 devices: a whole 4x8x12 slice. The times are simulated.
768 devices in a mesh: grp: 24 (over z, core), dev: 32 (over x, y).
Axes of the slice: x: 4, y: 8, z: 12, core: 2. Of those that a mesh axis runs over, the one named last changes fastest.
Arguments:
- positions: float32 [3, 3072, 544], P(None, ('grp', 'dev')), may hold values from -2 to 140, as said below
- rest_shape: float32 [3, 544], replicated, may hold values from -3 to 3
- stiffness: float32 [544, 544], replicated, may hold values from -0.25 to 0.25
- up_map: float32 [544, 152], replicated, may hold values from -0.25 to 0.25
- down_map: float32 [152, 544], replicated, may hold values from -0.5 to 0.5
- m2m: float32 [152, 152], replicated, may hold values from -0.5 to 0.5
- box_template: float32 [3, 152], replicated, may hold values from -1 to 1
- near_target: int32 [768, 2], P(('grp', 'dev')), may hold values from 0 to 3
- near_owner: int32 [768, 2], P(('grp', 'dev')), may hold values from 0 to 31, as said below
- near_cell: int32 [768, 2], P(('grp', 'dev')), may hold values from 0 to 3, as said below
- near_count: int32 [768], P(('grp', 'dev')), may hold values from 1 to 2, as said below
Outputs:
- new_positions: float32 [3, 3072, 544], P(None, ('grp', 'dev'))
- velocity: float32 [3, 3072, 544], P(None, ('grp', 'dev'))
Inputs may be any that keep to these rules, and one draw needn't show every extreme that they name: `positions`: each cell's points lie within about 1.2 of the cell's center; devices of one group sit on a grid of spacing 2.5, groups are 6 apart. `near_owner`: device e's slots name devices of e's own group other than e itself; at most 2 used slots of one device name the same owner, and device 0 uses all 2 slots with exactly 2 on each owner it names. `near_cell`: the source cells named by one device's used slots are distinct. `near_count`: the used slots come first; device 0 uses all of them.
All inputs are finite; a program needn't handle non-finite values.
Results may differ from a plain program's by a relative error of at most 0.0003.
Values sent between devices are 32-bit elements; how exact they have to be, the bound alone decides.
A program may use at most 32 MiB of HBM per device.

v0:
```python
import jax
import jax.numpy as jnp
from jax import lax
from jax.sharding import PartitionSpec as P

NEAR = 2
CAP = 2
STEPS = 2


EPSILON_SQ = 0.25
VISCOSITY = 0.039788735772973836
TIME_STEP = 0.1
SKALAK_HARDEN = 2.0
CHECK_RADIUS = 1.0
DEVICE_RADIUS = 1.5
GROUP_RADIUS = 6.0


def side_by_side(arrays, axis, dim, along):
    columns = [a.reshape(*a.shape[:along], -1) for a in arrays]
    both = jnp.concatenate(columns, axis=along)
    filled, at, gathered = (lax.all_gather(both, axis, axis=dim, tiled=True), 0, [])
    for a, column in zip(arrays, columns):
        section = filled[..., at : at + column.shape[along]]
        gathered.append(section.reshape(*section.shape[:along], *a.shape[along:]))
        at += column.shape[along]
    return tuple(gathered)


def stokes(targets, sources, forces):
    delta_x = targets[0][:, None] - sources[0][None, :]
    delta_y = targets[1][:, None] - sources[1][None, :]
    delta_z = targets[2][:, None] - sources[2][None, :]
    square = delta_x * delta_x + delta_y * delta_y + delta_z * delta_z
    inverse = 1.0 / ((square + EPSILON_SQ) * jnp.sqrt(square + EPSILON_SQ))
    direct = (square + 2.0 * EPSILON_SQ) * inverse
    projected = (
        delta_x * forces[0][None, :] + delta_y * forces[1][None, :] + delta_z * forces[2][None, :]
    ) * inverse
    result = jnp.einsum("ts,ks->kt", direct, forces, precision=lax.Precision.HIGHEST)
    extra = jnp.stack(
        [
            jnp.sum(delta_x * projected, axis=1),
            jnp.sum(delta_y * projected, axis=1),
            jnp.sum(delta_z * projected, axis=1),
        ]
    )
    return VISCOSITY * (result + extra)


def membrane(points, rest_shape, stiffness):
    centroid = jnp.mean(points, axis=2, keepdims=True)
    strain = points - centroid - rest_shape[:, None, :]
    linear = jnp.dot(
        strain.reshape(-1, strain.shape[2]), stiffness, precision=lax.Precision.HIGHEST
    ).reshape(strain.shape)
    stretch = jnp.sum(linear * linear, axis=0)
    return -linear * (1.0 + SKALAK_HARDEN * stretch / (1.0 + stretch))


def box_far(checks, equivalents, centers, radius, weights, box_template):
    sources = centers[:, :, None] + radius * box_template[None]
    forces = equivalents * weights.astype(equivalents.dtype)[:, None, None]
    source_count = equivalents.shape[0] * equivalents.shape[2]
    flat_sources = jnp.transpose(sources, (1, 0, 2)).reshape(3, source_count)
    flat_forces = jnp.transpose(forces, (1, 0, 2)).reshape(3, source_count)
    return stokes(checks, flat_sources, flat_forces)


def body(
    positions,
    rest_shape,
    stiffness,
    up_map,
    down_map,
    m2m,
    box_template,
    near_target,
    near_owner,
    near_cell,
    near_count,
):
    own_device = lax.axis_index("dev")
    own_group = lax.axis_index("grp")
    dev_count = lax.axis_size("dev")
    cell_count = positions.shape[1]
    surface = positions.shape[2]
    slot_ids = jnp.arange(NEAR, dtype=jnp.int32)
    owners = near_owner[0]
    cell_ids = near_cell[0]
    targets = near_target[0]
    in_use = slot_ids < near_count[0]
    onehot = (
        (targets[:, None] == jnp.arange(cell_count, dtype=jnp.int32)[None, :]) & in_use[:, None]
    ).astype(jnp.float32)
    earlier = (
        (owners[:, None] == owners[None, :])
        & in_use[None, :]
        & (slot_ids[None, :] < slot_ids[:, None])
    )
    slot_rank = jnp.sum(earlier.astype(jnp.int32), axis=1)
    matched = (
        (jnp.arange(dev_count, dtype=jnp.int32)[:, None, None] == owners[None, None, :])
        & (jnp.arange(CAP, dtype=jnp.int32)[None, :, None] == slot_rank[None, None, :])
        & in_use[None, None, :]
    )
    request = jnp.sum(matched.astype(jnp.int32) * (cell_ids + 1)[None, None, :], axis=2) - 1
    incoming = jnp.maximum(
        lax.all_to_all(request, "dev", split_axis=0, concat_axis=0, tiled=True), 0
    )
    source_rows = owners * CAP + slot_rank
    points = positions
    velocity = jnp.zeros_like(positions)
    for step_index in range(STEPS):
        forces = membrane(points, rest_shape, stiffness)
        stacked = jnp.concatenate([points, forces], axis=0)
        picked = jnp.take(stacked, incoming, axis=1)
        arrived = lax.all_to_all(picked, "dev", split_axis=1, concat_axis=1, tiled=True)
        source_pool = arrived.reshape(6, dev_count * CAP, surface)
        sources = jnp.take(source_pool, source_rows, axis=1)
        receivers = jnp.take(points, targets, axis=1)
        near_tiles = jax.vmap(stokes, in_axes=(1, 1, 1), out_axes=1)(
            receivers, sources[:3], sources[3:]
        )
        near_velocity = jnp.einsum(
            "ksp,sc->kcp", near_tiles, onehot, precision=lax.Precision.HIGHEST
        )
        equivalent = jnp.dot(jnp.sum(forces, axis=1), up_map, precision=lax.Precision.HIGHEST)
        center = jnp.mean(points, axis=(1, 2))
        checks = center[:, None] + CHECK_RADIUS * box_template
        box_forces, places = side_by_side((equivalent[None], center[None]), "dev", 0, 2)
        indices = jnp.arange(box_forces.shape[0], dtype=jnp.int32)
        added = box_far(
            checks, box_forces, places, DEVICE_RADIUS, indices != own_device, box_template
        )
        equivalent_sum = jnp.sum(box_forces, axis=0)
        center_sum = jnp.sum(places, axis=0)
        group_eq = jnp.dot(equivalent_sum, m2m, precision=lax.Precision.HIGHEST)
        group_center = center_sum / dev_count
        outer_box_forces, outer_places = side_by_side(
            (group_eq[None], group_center[None]), "grp", 0, 2
        )
        outer_indices = jnp.arange(outer_box_forces.shape[0], dtype=jnp.int32)
        outer_far = box_far(
            checks,
            outer_box_forces,
            outer_places,
            GROUP_RADIUS,
            outer_indices != own_group,
            box_template,
        )
        far_checks = added + outer_far
        far_surface = jnp.dot(far_checks, down_map, precision=lax.Precision.HIGHEST)
        velocity = far_surface[:, None, :] + near_velocity
        points = points + TIME_STEP * velocity
    return (points, velocity)


def solution(mesh):
    return jax.shard_map(
        body,
        mesh=mesh,
        in_specs=(
            P(None, ("grp", "dev"), None),
            P(),
            P(),
            P(),
            P(),
            P(),
            P(),
            P(("grp", "dev"), None),
            P(("grp", "dev"), None),
            P(("grp", "dev"), None),
            P(("grp", "dev")),
        ),
        out_specs=(P(None, ("grp", "dev"), None), P(None, ("grp", "dev"), None)),
        check_vma=False,
    )
```

profile of v0, /device:TPU:8, one launch (start us, length us, event | category | flops | bytes accessed | tf_op | source)
XLA Modules:
  0.0 267.9 jit_solution(2582988045142650379)
XLA Ops:
  2.2 0.9 fusion.203
  4.6 12.9 %all-to-all-start = ((s32[32,1,2]{2,1,0:T(1,128)}), s32[32,1,2]{2,1,0:T(1,128)S(1)}, u32[]{:S(2)}, u32[]{:S(2)}) async-start(s32[32,1,2]{2,1,0:T(1,128)} %copy.104), calls=%async_computation | async-start | bytes 32768 | tf_op jit(solution)/shard_map/all_to_all | solution.py:110
  17.5 0.9 fusion.229
  18.4 1.7 multiply_reduce_fusion.1
  20.8 38.9 %all_gather.12 = f32[32,3,153]{2,1,0:T(4,128)S(1)} all-gather(f32[1,3,153]{2,1,0:T(4,128)S(1)} %pad_maximum_fusion.2), channel_id=1, replica_groups=mesh['grp'=24,'dev'=32] {'dev'}, dimensions={0}, use_global_device_ids=true | all-gather | bytes 60588 | tf_op jit(solution)/shard_map/all_gather | solution.py:23
  60.8 30.8 %all_gather.13 = f32[24,3,153]{2,1,0:T(4,128)S(1)} all-gather(f32[1,3,153]{2,1,0:T(4,128)S(1)} %pad_maximum_fusion.3), channel_id=1, replica_groups=mesh['grp'=24,'dev'=32] {'grp'}, dimensions={0}, use_global_device_ids=true | all-gather | bytes 45900 | tf_op jit(solution)/shard_map/all_gather | solution.py:23
  94.9 4.3 %fusion.7 = (f32[152]{0:T(256)S(1)}, f32[152]{0:T(256)S(1)}, f32[152]{0:T(256)S(1)}) fusion(f32[4864]{0:T(1024)S(1)} %sub.336, f32[152]{0:T(256)S(1)} %bitcast.221, f32[4864]{0:T(1024)S(1)} %mul.474, f32[4864]{0:T(1024)S(1)} %sub.346, f32[152]{0:T(256)S(1)} %bitcast.225, f32[4864]{0:T(1024)S(1)} %mul.471, f32[4864]{0:T(1024)S(1)} %sub.341, ...), kind=kLoop, calls=%fused_computation.73 | loop fusion | flops 17004088 | bytes 120384 | tf_op jit(solution)/shard_map/reduce_sum | solution.py:44
  99.2 5.0 %fusion.176 = f32[3,152]{1,0:T(4,128)} fusion(f32[3,4864]{1,0:T(4,128)S(1)} %reshape.284, f32[4864]{0:T(1024)S(1)} %sub.346, f32[152]{0:T(256)S(1)} %bitcast.226, f32[4864]{0:T(1024)S(1)} %sub.341, f32[152]{0:T(256)S(1)} %bitcast.230, f32[4864]{0:T(1024)S(1)} %sub.336, f32[152]{0:T(256)S(1)} %bitcast.222, f32[1,152]{1,0:T(1,128)S(1)} %bitcast.242, ...), kind=kOutput, calls=%fused_computation.212 | convolution fusion | flops 36228440 | bytes 122208 | tf_op jit(solution)/shard_map/ts,ks->kt/dot_general | solution.py:41
  105.9 1.6 fusion.183
  107.5 8.3 %all-to-all-start.1 = ((f32[6,32,2,544]{3,2,0,1:T(2,128)}), f32[6,32,2,544]{3,2,0,1:T(2,128)S(1)}, u32[]{:S(2)}, u32[]{:S(2)}) async-start(f32[6,32,2,544]{3,2,0,1:T(2,128)} %fusion.183), calls=%async_computation.1 | async-start | bytes 1966080 | tf_op jit(solution)/shard_map/all_to_all | solution.py:119
  115.9 3.1 %fusion.63 = (f32[152]{0:T(256)S(1)}, f32[152]{0:T(256)S(1)}, f32[152]{0:T(256)S(1)}) fusion(f32[3648]{0:T(1024)S(1)} %sub.350, f32[152]{0:T(256)S(1)} %bitcast.223, f32[3648]{0:T(1024)S(1)} %mul.496, f32[3648]{0:T(1024)S(1)} %sub.358, f32[152]{0:T(256)S(1)} %bitcast.227, f32[3648]{0:T(1024)S(1)} %mul.493, f32[3648]{0:T(1024)S(1)} %sub.354, ...), kind=kLoop, calls=%fused_computation.125 | loop fusion | flops 12752952 | bytes 91200 | tf_op jit(solution)/shard_map/reduce_sum | solution.py:44
  119.0 3.4 %fusion.164 = f32[3,152]{1,0:T(4,128)S(1)} fusion(f32[3,152]{1,0:T(4,128)S(1)} %copy-done.30, f32[3,3648]{1,0:T(4,128)S(1)} %reshape.285, f32[3648]{0:T(1024)S(1)} %sub.358, f32[152]{0:T(256)S(1)} %bitcast.228, f32[3648]{0:T(1024)S(1)} %sub.354, f32[152]{0:T(256)S(1)} %bitcast.232, f32[3648]{0:T(1024)S(1)} %sub.350, f32[152]{0:T(256)S(1)} %bitcast.224, ...), kind=kOutput, calls=%fused_computation.208 | convolution fusion | flops 27172584 | bytes 94848 | tf_op jit(solution)/shard_map/ts,ks->kt/dot_general | solution.py:41
  122.7 20.2 %all-to-all-done.1 = f32[6,32,2,544]{3,2,0,1:T(2,128)S(1)} async-done(((f32[6,32,2,544]{3,2,0,1:T(2,128)}), f32[6,32,2,544]{3,2,0,1:T(2,128)S(1)}, u32[]{:S(2)}, u32[]{:S(2)}) %all-to-all-start.1) | async-done | bytes 835616 | tf_op jit(solution)/shard_map/all_to_all | solution.py:119
  142.9 1.2 copy.110
  144.2 1.9 gather_fusion.1
  146.2 4.6 %fusion.35 = (f32[2,544]{1,0:T(2,128)S(1)}, f32[2,544]{1,0:T(2,128)S(1)}, f32[2,544]{1,0:T(2,128)S(1)}) fusion(f32[2,544]{1,0:T(2,128)S(1)} %get-tuple-element.108, f32[2,544]{1,0:T(2,128)S(1)} %get-tuple-element.80, f32[2,544]{1,0:T(2,128)S(1)} %get-tuple-element.103, f32[2,544]{1,0:T(2,128)S(1)} %get-tuple-element.106, f32[2,544]{1,0:T(2,128)S(1)} %get-tuple-element.81, ...), kind=kLoop, calls=%fused_computation.99 | loop fusion | flops 13609792 | bytes 52224 | tf_op jit(solution)/shard_map/vmap()/reduce_sum | solution.py:44
  150.9 4.6 %fusion.155 = f32[3,2,544]{2,0,1:T(4,128)S(1)} fusion(f32[2,544]{1,0:T(2,128)S(1)} %get-tuple-element.106, f32[2,544]{1,0:T(2,128)S(1)} %get-tuple-element.81, f32[2,544]{1,0:T(2,128)S(1)} %get-tuple-element.107, f32[2,544]{1,0:T(2,128)S(1)} %get-tuple-element.82, f32[2,544]{1,0:T(2,128)S(1)} %get-tuple-element.108, f32[2,544]{1,0:T(2,128)S(1)} %get-tuple-element.80, ...), kind=kOutput, calls=%fused_computation.201 | convolution fusion | flops 29014784 | bytes 79616 | tf_op jit(solution)/shard_map/vmap(ts,ks->kt)/dot_general | solution.py:41
  155.9 0.9 multiply_reduce_fusion
  157.5 36.1 %all_gather.14 = f32[32,3,153]{2,1,0:T(4,128)S(1)} all-gather(f32[1,3,153]{2,1,0:T(4,128)S(1)} %pad_maximum_fusion.4), channel_id=1, replica_groups=mesh['grp'=24,'dev'=32] {'dev'}, dimensions={0}, use_global_device_ids=true | all-gather | bytes 60588 | tf_op jit(solution)/shard_map/all_gather | solution.py:23
  194.3 20.7 %all_gather.15 = f32[24,3,153]{2,1,0:T(4,128)S(1)} all-gather(f32[1,3,153]{2,1,0:T(4,128)S(1)} %pad_maximum_fusion.5), channel_id=1, replica_groups=mesh['grp'=24,'dev'=32] {'grp'}, dimensions={0}, use_global_device_ids=true | all-gather | bytes 45900 | tf_op jit(solution)/shard_map/all_gather | solution.py:23
  217.5 1.6 fusion.182
  219.1 7.6 %all-to-all-start.2 = ((f32[6,32,2,544]{3,2,0,1:T(2,128)}), f32[6,32,2,544]{3,2,0,1:T(2,128)S(1)}, u32[]{:S(2)}, u32[]{:S(2)}) async-start(f32[6,32,2,544]{3,2,0,1:T(2,128)} %fusion.182), calls=%async_computation.2 | async-start | bytes 1966080 | tf_op jit(solution)/shard_map/all_to_all | solution.py:119
  227.5 4.5 %fusion.18 = (f32[152]{0:T(256)S(1)}, f32[152]{0:T(256)S(1)}, f32[152]{0:T(256)S(1)}) fusion(f32[4864]{0:T(1024)S(1)} %sub.383, f32[152]{0:T(256)S(1)} %bitcast.209, f32[4864]{0:T(1024)S(1)} %mul.544, f32[4864]{0:T(1024)S(1)} %sub.393, f32[152]{0:T(256)S(1)} %bitcast.213, f32[4864]{0:T(1024)S(1)} %mul.541, f32[4864]{0:T(1024)S(1)} %sub.388, ...), kind=kLoop, calls=%fused_computation.84 | loop fusion | flops 17004088 | bytes 120384 | tf_op jit(solution)/shard_map/reduce_sum | solution.py:44
  232.1 4.4 %fusion.179 = f32[3,152]{1,0:T(4,128)S(1)} fusion(f32[3,4864]{1,0:T(4,128)S(1)} %reshape.287, f32[4864]{0:T(1024)S(1)} %sub.393, f32[152]{0:T(256)S(1)} %bitcast.214, f32[4864]{0:T(1024)S(1)} %sub.388, f32[152]{0:T(256)S(1)} %bitcast.218, f32[4864]{0:T(1024)S(1)} %sub.383, f32[152]{0:T(256)S(1)} %bitcast.210, f32[1,152]{1,0:T(1,128)S(1)} %bitcast.245, ...), kind=kOutput, calls=%fused_computation.213 | convolution fusion | flops 36228440 | bytes 122208 | tf_op jit(solution)/shard_map/ts,ks->kt/dot_general | solution.py:41
  237.5 3.1 %fusion.74 = (f32[152]{0:T(256)S(1)}, f32[152]{0:T(256)S(1)}, f32[152]{0:T(256)S(1)}) fusion(f32[3648]{0:T(1024)S(1)} %sub.397, f32[152]{0:T(256)S(1)} %bitcast.211, f32[3648]{0:T(1024)S(1)} %mul.564, f32[3648]{0:T(1024)S(1)} %sub.405, f32[152]{0:T(256)S(1)} %bitcast.215, f32[3648]{0:T(1024)S(1)} %mul.561, f32[3648]{0:T(1024)S(1)} %sub.401, ...), kind=kLoop, calls=%fused_computation.136 | loop fusion | flops 12752952 | bytes 91200 | tf_op jit(solution)/shard_map/reduce_sum | solution.py:44
  240.6 3.4 %fusion.173 = f32[3,152]{1,0:T(4,128)S(1)} fusion(f32[3,152]{1,0:T(4,128)S(1)} %fusion.179, f32[3,3648]{1,0:T(4,128)S(1)} %reshape.288, f32[3648]{0:T(1024)S(1)} %sub.405, f32[152]{0:T(256)S(1)} %bitcast.216, f32[3648]{0:T(1024)S(1)} %sub.401, f32[152]{0:T(256)S(1)} %bitcast.220, f32[3648]{0:T(1024)S(1)} %sub.397, f32[152]{0:T(256)S(1)} %bitcast.212, ...), kind=kOutput, calls=%fused_computation.211 | convolution fusion | flops 27172584 | bytes 94848 | tf_op jit(solution)/shard_map/ts,ks->kt/dot_general | solution.py:41
  244.3 9.7 %all-to-all-done.2 = f32[6,32,2,544]{3,2,0,1:T(2,128)S(1)} async-done(((f32[6,32,2,544]{3,2,0,1:T(2,128)}), f32[6,32,2,544]{3,2,0,1:T(2,128)S(1)}, u32[]{:S(2)}, u32[]{:S(2)}) %all-to-all-start.2) | async-done | bytes 835616 | tf_op jit(solution)/shard_map/all_to_all | solution.py:119
  254.0 1.2 copy.122
  255.2 2.0 gather_fusion.4
  257.4 4.7 %fusion.46 = (f32[2,544]{1,0:T(2,128)S(1)}, f32[2,544]{1,0:T(2,128)S(1)}, f32[2,544]{1,0:T(2,128)S(1)}) fusion(f32[2,544]{1,0:T(2,128)S(1)} %bitcast.202, f32[2,544]{1,0:T(2,128)S(1)} %bitcast.196, f32[2,544]{1,0:T(2,128)S(1)} %bitcast.204, f32[2,544]{1,0:T(2,128)S(1)} %bitcast.198, f32[2,544]{1,0:T(2,128)S(1)} %bitcast.192, f32[2,544]{1,0:T(2,128)S(1)} %bitcast.205, ...), kind=kLoop, calls=%fused_computation.110 | loop fusion | flops 13609792 | bytes 52224 | tf_op jit(solution)/shard_map/vmap()/reduce_sum | solution.py:44
  262.1 4.6 %fusion.149 = f32[3,2,544]{2,0,1:T(4,128)S(1)} fusion(f32[2,544]{1,0:T(2,128)S(1)} %bitcast.199, f32[2,544]{1,0:T(2,128)S(1)} %bitcast.193, f32[2,544]{1,0:T(2,128)S(1)} %bitcast.201, f32[2,544]{1,0:T(2,128)S(1)} %bitcast.195, f32[2,544]{1,0:T(2,128)S(1)} %bitcast.203, f32[2,544]{1,0:T(2,128)S(1)} %bitcast.197, f32[6,2,544]{2,0,1:T(8,128)S(1)} %select_bitcast_fusion, ...), kind=kOutput, calls=%fused_computation.199 | convolution fusion | flops 29014784 | bytes 79616 | tf_op jit(solution)/shard_map/vmap(ts,ks->kt)/dot_general | solution.py:41
  266.7 0.9 multiply_add_fusion
  (204 shorter events, 15.4 us)
Async XLA Ops:
  0.6 17.7 %copy-start = (f32[544,544]{1,0:T(8,128)S(1)}, f32[544,544]{1,0:T(8,128)}, u32[]{:S(2)}) copy-start(f32[544,544]{1,0:T(8,128)} %param.19) | copy-start | bytes 3551236
  0.6 19.6 %copy-start.1 = (f32[544,152]{0,1:T(8,128)S(1)}, f32[544,152]{0,1:T(8,128)}, u32[]{:S(2)}) copy-start(f32[544,152]{0,1:T(8,128)} %param.20) | copy-start | bytes 992260
  1.4 2.3 copy-start.20
  4.6 100.2 %all-to-all-start = ((s32[32,1,2]{2,1,0:T(1,128)}), s32[32,1,2]{2,1,0:T(1,128)S(1)}, u32[]{:S(2)}, u32[]{:S(2)}) async-start(s32[32,1,2]{2,1,0:T(1,128)} %copy.104), calls=%async_computation | async-start | bytes 32768 | tf_op jit(solution)/shard_map/all_to_all | solution.py:110
  18.4 42.2 %copy-start.5 = (f32[152,152]{1,0:T(8,128)S(1)}, f32[152,152]{1,0:T(8,128)}, u32[]{:S(2)}) copy-start(f32[152,152]{1,0:T(8,128)} %param.22) | copy-start | bytes 277252
  20.1 72.0 %copy-start.12 = (s32[1,2]{1,0:T(1,128)S(1)}, s32[1,2]{1,0:T(1,128)}, u32[]{:S(2)}) copy-start(s32[1,2]{1,0:T(1,128)} %param.25) | copy-start | bytes 28
  20.1 72.5 %copy-start.28 = (s32[1,2]{1,0:T(1,128)S(1)}, s32[1,2]{1,0:T(1,128)}, u32[]{:S(2)}) copy-start(s32[1,2]{1,0:T(1,128)} %param.24) | copy-start | bytes 28
  20.1 72.7 %copy-start.7 = (f32[3,152]{1,0:T(4,128)S(1)}, f32[3,152]{1,0:T(4,128)}, u32[]{:S(2)}) copy-start(f32[3,152]{1,0:T(4,128)} %param.23) | copy-start | bytes 5476
  60.0 34.1 %copy-start.4 = (f32[3,4,544]{2,1,0:T(4,128)S(1)}, f32[3,4,544]{2,1,0:T(4,128)}, u32[]{:S(2)}) copy-start(f32[3,4,544]{2,1,0:T(4,128)} %param.17) | copy-start | bytes 78340
  92.6 6.6 %copy-start.17 = (pred[2]{0:T(512)(128)(4,1)}, pred[2]{0:T(512)(128)(4,1)S(1)}, u32[]{:S(2)}) copy-start(pred[2]{0:T(512)(128)(4,1)S(1)} %compare_and_fusion) | copy-start | bytes 10
  93.6 10.7 %copy-start.22 = (f32[1,152]{1,0:T(1,128)}, f32[1,152]{1,0:T(1,128)S(1)}, u32[]{:S(2)}) copy-start(f32[1,152]{1,0:T(1,128)S(1)} %get-tuple-element.89) | copy-start | bytes 1828
  93.6 10.7 %copy-start.24 = (f32[1,152]{1,0:T(1,128)}, f32[1,152]{1,0:T(1,128)S(1)}, u32[]{:S(2)}) copy-start(f32[1,152]{1,0:T(1,128)S(1)} %get-tuple-element.90) | copy-start | bytes 1828
  93.6 10.7 %copy-start.26 = (f32[1,152]{1,0:T(1,128)}, f32[1,152]{1,0:T(1,128)S(1)}, u32[]{:S(2)}) copy-start(f32[1,152]{1,0:T(1,128)S(1)} %get-tuple-element.91) | copy-start | bytes 1828
  94.2 10.0 %copy-start.10 = (s32[1024]{0:T(1024)}, s32[1024]{0:T(1024)S(1)}, u32[]{:S(2)}) copy-start(s32[1024]{0:T(1024)S(1)} %pad_clamp_fusion) | copy-start | bytes 12292
  107.5 8.4 %copy-start.19 = (s32[2]{0:T(128)S(1)}, s32[2]{0:T(128)}, u32[]{:S(2)}) copy-start(s32[2]{0:T(128)} %get-tuple-element.44) | copy-start | bytes 28
  107.5 8.4 %copy-start.23 = (f32[1,152]{1,0:T(1,128)S(1)}, f32[1,152]{1,0:T(1,128)}, u32[]{:S(2)}) copy-start(f32[1,152]{1,0:T(1,128)} %copy-done.22) | copy-start | bytes 1828
  107.5 8.4 %copy-start.25 = (f32[1,152]{1,0:T(1,128)S(1)}, f32[1,152]{1,0:T(1,128)}, u32[]{:S(2)}) copy-start(f32[1,152]{1,0:T(1,128)} %copy-done.24) | copy-start | bytes 1828
  107.5 8.4 %copy-start.27 = (f32[1,152]{1,0:T(1,128)S(1)}, f32[1,152]{1,0:T(1,128)}, u32[]{:S(2)}) copy-start(f32[1,152]{1,0:T(1,128)} %copy-done.26) | copy-start | bytes 1828
  107.5 11.5 %copy-start.30 = (f32[3,152]{1,0:T(4,128)S(1)}, f32[3,152]{1,0:T(4,128)}, u32[]{:S(2)}) copy-start(f32[3,152]{1,0:T(4,128)} %fusion.176) | copy-start | bytes 5476
  107.5 35.5 %all-to-all-start.1 = ((f32[6,32,2,544]{3,2,0,1:T(2,128)}), f32[6,32,2,544]{3,2,0,1:T(2,128)S(1)}, u32[]{:S(2)}, u32[]{:S(2)}) async-start(f32[6,32,2,544]{3,2,0,1:T(2,128)} %fusion.183), calls=%async_computation.1 | async-start | bytes 1966080 | tf_op jit(solution)/shard_map/all_to_all | solution.py:119
  115.8 28.3 %copy-start.9 = (s32[1024]{0:T(1024)}, s32[1024]{0:T(1024)S(1)}, u32[]{:S(2)}) copy-start(s32[1024]{0:T(1024)S(1)} %pad_clamp_fusion.1) | copy-start | bytes 12292
  119.0 3.5 %copy-start.2 = (f32[152,544]{1,0:T(8,128)S(1)}, f32[152,544]{1,0:T(8,128)}, u32[]{:S(2)}) copy-start(f32[152,544]{1,0:T(8,128)} %param.21) | copy-start | bytes 992260
  122.4 23.6 %copy-start.11 = (pred[2]{0:T(512)(128)(4,1)S(1)}, pred[2]{0:T(512)(128)(4,1)}, u32[]{:S(2)}) copy-start(pred[2]{0:T(512)(128)(4,1)} %get-tuple-element.43) | copy-start | bytes 10
  150.8 4.6 %copy-start.21 = (pred[2]{0:T(512)(128)(4,1)S(1)}, pred[2]{0:T(512)(128)(4,1)}, u32[]{:S(2)}) copy-start(pred[2]{0:T(512)(128)(4,1)} %copy-done.20) | copy-start | bytes 10
  150.8 4.6 %copy-start.29 = (s32[1,2]{1,0:T(1,128)S(1)}, s32[1,2]{1,0:T(1,128)}, u32[]{:S(2)}) copy-start(s32[1,2]{1,0:T(1,128)} %param.24) | copy-start | bytes 28
  150.9 5.0 %copy-start.6 = (f32[3,544]{1,0:T(4,128)S(1)}, f32[3,544]{1,0:T(4,128)}, u32[]{:S(2)}) copy-start(f32[3,544]{1,0:T(4,128)} %param.18) | copy-start | bytes 19588
  155.4 38.2 %copy-start.14 = (f32[32]{0:T(128)S(1)}, f32[32]{0:T(128)}, u32[]{:S(2)}) copy-start(f32[32]{0:T(128)} %copy-done.13) | copy-start | bytes 388
  155.9 59.2 %copy-start.16 = (f32[24]{0:T(128)S(1)}, f32[24]{0:T(128)}, u32[]{:S(2)}) copy-start(f32[24]{0:T(128)} %copy-done.15) | copy-start | bytes 292
  156.8 59.0 %copy-start.8 = (f32[3,152]{1,0:T(4,128)S(1)}, f32[3,152]{1,0:T(4,128)}, u32[]{:S(2)}) copy-start(f32[3,152]{1,0:T(4,128)} %param.23) | copy-start | bytes 5476
  219.1 8.4 %copy-start.18 = (pred[2]{0:T(512)(128)(4,1)S(1)}, pred[2]{0:T(512)(128)(4,1)}, u32[]{:S(2)}) copy-start(pred[2]{0:T(512)(128)(4,1)} %copy-done.17) | copy-start | bytes 10
  219.1 34.9 %all-to-all-start.2 = ((f32[6,32,2,544]{3,2,0,1:T(2,128)}), f32[6,32,2,544]{3,2,0,1:T(2,128)S(1)}, u32[]{:S(2)}, u32[]{:S(2)}) async-start(f32[6,32,2,544]{3,2,0,1:T(2,128)} %fusion.182), calls=%async_computation.2 | async-start | bytes 1966080 | tf_op jit(solution)/shard_map/all_to_all | solution.py:119
  240.6 3.5 %copy-start.3 = (f32[152,544]{1,0:T(8,128)S(1)}, f32[152,544]{1,0:T(8,128)}, u32[]{:S(2)}) copy-start(f32[152,544]{1,0:T(8,128)} %param.21) | copy-start | bytes 992260
  (2 other events, 1.7 us)
where the time goes:
time: 271 us; the launch traced here: 268 us
  blocking collectives  127 us (47%)
  other arithmetic  33.4 us (12%)
  matrix products  31.1 us (11%)
  waiting for transfers between devices  29.9 us (11%)
  starting transfers between devices  28.9 us (11%)
  local copies, waits for them, and re-layouts  15.2 us (6%)
  between operations  2.81 us (1%)
    all_gather x4, blocking collectives, side_by_side(): lax.all_gather(both, axis, axis=dim, tiled=True)  127 us
    all_to_all x2, waiting for transfers between devices, body(): lax.all_to_all(picked, 'dev', split_axis=1, concat_axis=1, tiled=True)  29.9 us
    dot_general x6, matrix products, stokes(): jnp.einsum('ts,ks->kt', direct, forces, precision=lax.Precision.HIGHEST)  25.4 us
    reduce_sum x6, other arithmetic, stokes(): jnp.sum(delta_x * projected, axis=1)  24.2 us
    all_to_all x2, starting transfers between devices, body(): lax.all_to_all(picked, 'dev', split_axis=1, concat_axis=1, tiled=True)  16 us
    all_to_all x1, starting transfers between devices, body(): lax.all_to_all(request, 'dev', split_axis=0, concat_axis=0, tiled=True)  12.9 us
  transfers between devices with their start and end apart: 3, of which 2 were waited for; matrix products, arithmetic and copies ran while one was open for 15% of the time, Pallas kernels for 0%

commit v1 on v0

v1 whole, which is shorter than its diff:
```python
import functools

import jax
import jax.numpy as jnp
from jax import lax
from jax.experimental import pallas as pl
from jax.experimental.pallas import tpu as pltpu
from jax.sharding import PartitionSpec as P

STEPS = 2
EPS = 0.25
VISCOSITY = 0.039788735772973836
TIME_STEP = 0.1
SKALAK_HARDEN = 2.0
CHECK_RADIUS = 1.0
DEVICE_RADIUS = 1.5
GROUP_RADIUS = 6.0

NG = 24
ND = 32
NX = 4
NY = 8
PT = 544
PP = 640
Q = 152
F32 = jnp.float32
BF = jnp.bfloat16
MESH = pl.DeviceIdType.MESH

EQ, GP, CA, CB, RQ = 0, 2, 4, 6, 8


def halves(w):
    hi = w.astype(BF)
    return hi, (w - hi.astype(F32)).astype(BF)


def dot(a, b):
    return jnp.dot(a, b, preferred_element_type=F32)


def mm(a, hi, lo):
    ah, al = halves(a)
    return dot(ah, hi[...]) + dot(al, hi[...]) + dot(ah, lo[...])


def pair(t, s, acc):
    tx, ty, tz = t
    sx, sy, sz, fx, fy, fz = s
    dx, dy, dz = tx - sx, ty - sy, tz - sz
    rs = lax.rsqrt(dx * dx + dy * dy + (dz * dz + EPS))
    b = rs * rs * rs
    direct = rs + EPS * b
    proj = (dx * fx + dy * fy + dz * fz) * b
    return (
        acc[0] + (direct * fx + proj * dx),
        acc[1] + (direct * fy + proj * dy),
        acc[2] + (direct * fz + proj * dz),
    )


def row_of(tile, j, rows):
    return jnp.broadcast_to(tile[j : j + 1, :], (rows, 128))


def kernel(
    near_target,
    near_owner,
    near_cell,
    near_count,
    pos_ref,
    rest_ref,
    stiff_ref,
    up_ref,
    m2m_ref,
    down_ref,
    cols_ref,
    rows_ref,
    new_ref,
    vel_ref,
    st_hi,
    st_lo,
    up_hi,
    up_lo,
    mm_hi,
    mm_lo,
    dn_hi,
    dn_lo,
    targets,
    acc_ref,
    eq_buf,
    gp_buf,
    ca_buf,
    cb_send,
    cb_recv,
    rq_send,
    rq_recv,
    src_dev,
    src_grp,
    near_src,
    near_rows,
    near_cols,
    near_acc,
    send_sem,
    recv_sem,
):
    me = lax.axis_index("dev")
    grp = lax.axis_index("grp")
    mx = me // NY
    my = me % NY

    barrier = pltpu.get_barrier_semaphore()

    def greet(axis, own, count):
        def one(i, c):
            pl.semaphore_signal(
                barrier, inc=1, device_id={axis: lax.rem(own + i, count)}, device_id_type=MESH
            )
            return c

        lax.fori_loop(1, count, one, 0)

    greet("dev", me, ND)
    greet("grp", grp, NG)

    def push(src, dst, sem, device):
        pltpu.make_async_remote_copy(
            src_ref=src,
            dst_ref=dst,
            send_sem=send_sem.at[sem],
            recv_sem=recv_sem.at[sem],
            device_id=device,
            device_id_type=MESH,
        ).start()

    def arrived(ref, sem):
        pltpu.make_async_copy(ref, ref, recv_sem.at[sem]).wait()

    def left(ref, sem):
        pltpu.make_async_copy(ref, ref, send_sem.at[sem]).wait()

    def push_all(buf, base, rows, axis, own, count, sem):
        slot = buf.at[pl.ds(pl.multiple_of(base + own * rows, 8), rows), :]

        def one(i, c):
            push(slot, slot, sem, {axis: lax.rem(own + i, count)})
            return c

        lax.fori_loop(1, count, one, 0)

    st_hi[...], st_lo[...] = halves(stiff_ref[...])
    up_hi[...], up_lo[...] = halves(up_ref[...])
    mm_hi[...], mm_lo[...] = halves(m2m_ref[...])
    dn_hi[...], dn_lo[...] = halves(down_ref[...])
    for k in range(3):
        targets[k * Q : (k + 1) * Q, :] = jnp.broadcast_to(
            CHECK_RADIUS * cols_ref[:, k : k + 1], (Q, 128)
        )
    near_src[...] = jnp.zeros_like(near_src)
    near_rows[...] = jnp.zeros_like(near_rows)
    near_acc[...] = jnp.zeros_like(near_acc)

    sub = lax.broadcasted_iota(jnp.int32, (8, 128), 0)
    lane = lax.broadcasted_iota(jnp.int32, (8, 128), 1)
    row8 = lax.broadcasted_iota(jnp.int32, (8, PT), 0)
    count = near_count[0]
    t_of = [near_target[0, s] for s in range(2)]
    used = [s < count for s in range(2)]

    want, from_y = [], []
    for s in range(2):
        owner = near_owner[0, s]
        want.append((owner // NY) * 16 + near_cell[0, s])
        from_y.append(jnp.where(used[s], owner % NY, -1))
    kk = sub % 4
    slot_want = jnp.where(sub < 4, want[0], want[1]) + 4 * kk
    slot_y = jnp.where(sub < 4, from_y[0], from_y[1])
    for y in range(NY):
        rq_send[y * 8 : (y + 1) * 8, :] = jnp.where((slot_y == y) & (kk < 3), slot_want, -1)

    def membrane(pts):
        cents, strain = [], []
        for k in range(3):
            c = jnp.sum(pts[k], axis=1, keepdims=True) * (1.0 / PT)
            cents.append(c)
            strain.append(pts[k] - c - rest_ref[k : k + 1, :])
        flat = jnp.concatenate(strain, axis=0)
        hi = flat.astype(BF).astype(F32)
        both = jnp.concatenate([hi, flat - hi], axis=0).astype(BF)
        first = dot(both, st_hi[...])
        linear = first[:24] + first[24:] + dot(both[:32], st_lo[...])[:24]
        lin = [linear[8 * k : 8 * k + 8] for k in range(3)]
        stretch = lin[0] * lin[0] + lin[1] * lin[1] + lin[2] * lin[2]
        harden = 1.0 + SKALAK_HARDEN * stretch / (1.0 + stretch)
        return cents, [-l * harden for l in lin]

    def own_cells(pts):
        return jnp.concatenate([p[:4] for p in pts] + [jnp.zeros((4, PT), F32)], axis=0)

    def sources(src, buf, base, boxes, rem_rows, own, radius, center):
        total = boxes + 8
        mine = lax.broadcasted_iota(jnp.int32, (boxes, 128), 0) == own
        middle = buf[pl.ds(base + 6, boxes, stride=8), :]
        for k in range(3):
            f = buf[pl.ds(base + k, boxes, stride=8), :]
            src[(3 + k) * total : (3 + k) * total + boxes, :] = jnp.where(mine, 0.0, f * VISCOSITY)
            r = buf[pl.ds(base + 3 + k, boxes, stride=8), :]
            r = jnp.where(mine, 0.0, r * VISCOSITY)
            packed = r[0:8]
            for j in range(1, boxes // 8):
                packed = packed + r[8 * j : 8 * j + 8]
            src[(3 + k) * total + boxes : (4 + k) * total, :] = packed
            c = jnp.broadcast_to(middle[:, k : k + 1] - center[k], (boxes, 128))
            src[k * total : k * total + boxes, :] = c + radius * rows_ref[k : k + 1, :128]
            pc = c[0:8]
            for j in range(1, boxes // 8):
                pc = jnp.where(lane // 32 == j, c[8 * j : 8 * j + 8], pc)
            src[k * total + boxes : (k + 1) * total, :] = pc + radius * rows_ref[k : k + 1, 128:]

    def far(src, boxes, first):
        total = boxes + 8
        edges = [0, 24, 48, 72, 96, 120, 152]
        for lo, hi in zip(edges[:-1], edges[1:]):
            n = hi - lo
            t = [targets[k * Q + lo : k * Q + hi, :] for k in range(3)]
            if first:
                acc = tuple(jnp.zeros((n, 128), F32) for k in range(3))
            else:
                acc = tuple(acc_ref[k * Q + lo : k * Q + hi, :] for k in range(3))

            def one(c, acc):
                tiles = [
                    src[pl.ds(pl.multiple_of(k * total + c * 8, 8), 8), :] for k in range(6)
                ]
                for j in range(8):
                    acc = pair(t, [row_of(x, j, n) for x in tiles], acc)
                return acc

            acc = lax.fori_loop(0, total // 8, one, acc)
            for k in range(3):
                acc_ref[k * Q + lo : k * Q + hi, :] = acc[k]

    pts = [pos_ref[8 * k : 8 * k + 8, :] for k in range(3)]
    for step in range(STEPS):
        eq0, gp0, ca0, cb0 = step * 256, step * 192, step * 64, step * 64
        cents, forces = membrane(pts)
        center = [jnp.sum(c[:4], axis=0, keepdims=True) * 0.25 for c in cents]
        total = [jnp.sum(f[:4], axis=0, keepdims=True) for f in forces]
        m3 = row8 % 3
        fs = jnp.where(m3 == 0, total[0], jnp.where(m3 == 1, total[1], total[2]))
        e = mm(fs, up_hi, up_lo)
        mid = jnp.where(lane == 0, center[0], jnp.where(lane == 1, center[1], center[2]))
        msg = jnp.where(
            sub < 3,
            e[:, :128],
            jnp.where(
                sub < 6,
                jnp.where(lane // 32 == mx, e[:, 128:], 0.0),
                jnp.where(sub == 6, mid, 0.0),
            ),
        )
        eq_buf[pl.ds(pl.multiple_of(eq0 + me * 8, 8), 8), :] = msg
        ca_buf[pl.ds(pl.multiple_of(ca0 + mx * 16, 8), 16), :] = own_cells(pts)

        if step == 0:
            pl.semaphore_wait(barrier, ND - 1 + NG - 1)
        push_all(eq_buf, eq0, 8, "dev", me, ND, EQ + step)

        cells = ca_buf.at[pl.ds(pl.multiple_of(ca0 + mx * 16, 8), 16), :]
        for i in range(1, NX):
            push(cells, cells, CA + step, {"dev": lax.rem(mx + i, NX) * NY + my})
        mine = pl.ds(pl.multiple_of(my * 8, 8), 8)
        if step == 0:
            for i in range(1, NY):
                y = lax.rem(my + i, NY)
                push(
                    rq_send.at[pl.ds(pl.multiple_of(y * 8, 8), 8), :],
                    rq_recv.at[mine, :],
                    RQ,
                    {"dev": mx * NY + y},
                )
            rq_recv[mine, :] = rq_send[mine, :]
            arrived(rq_recv.at[pl.ds(0, 56), :], RQ)

        arrived(ca_buf.at[pl.ds(ca0, 48), :], CA + step)
        pick = rq_recv[:, :64] == lax.broadcasted_iota(jnp.int32, (64, 64), 1)
        pick = jnp.where(pick, 1.0, 0.0).astype(BF)
        cells = ca_buf[ca0 : ca0 + 64, :]
        c1 = cells.astype(BF)
        cells = cells - c1.astype(F32)
        c2 = cells.astype(BF)
        c3 = (cells - c2.astype(F32)).astype(BF)
        cb_send[cb0 : cb0 + 64, :] = (dot(pick, c1) + dot(pick, c2)) + dot(pick, c3)
        own_b = pl.ds(pl.multiple_of(cb0 + my * 8, 8), 8)
        for i in range(1, NY):
            y = lax.rem(my + i, NY)
            push(
                cb_send.at[pl.ds(pl.multiple_of(cb0 + y * 8, 8), 8), :],
                cb_recv.at[own_b, :],
                CB + step,
                {"dev": mx * NY + y},
            )
        cb_recv[own_b, :] = cb_send[own_b, :]

        arrived(eq_buf.at[pl.ds(eq0, 248), :], EQ + step)
        parts = [eq_buf[eq0 + 8 * i : eq0 + 8 * i + 8, :] for i in range(ND)]
        while len(parts) > 1:
            parts = [a + b for a, b in zip(parts[::2], parts[1::2])]
        tile = parts[0]
        th, tl = halves(tile)
        up1 = dot(th, mm_hi[:128]) + dot(tl, mm_hi[:128]) + dot(th, mm_lo[:128])
        up2 = dot(th, mm_hi[128:]) + dot(tl, mm_hi[128:]) + dot(th, mm_lo[128:])
        main = up1[:, :128] + pltpu.roll(up2[:, :128], 5, 0)
        rest = pltpu.roll(up1[:, 128:], 3, 0) + up2[:, 128:]
        msg = jnp.where(
            sub < 3,
            main,
            jnp.where(
                sub < 6, jnp.where(lane // 32 == grp // 8, rest, 0.0), tile * (1.0 / ND)
            ),
        )
        gp_buf[pl.ds(pl.multiple_of(gp0 + grp * 8, 8), 8), :] = msg
        push_all(gp_buf, gp0, 8, "grp", grp, NG, GP + step)

        sources(src_dev, eq_buf, eq0, ND, 8, me, DEVICE_RADIUS, center)
        far(src_dev, ND, True)

        arrived(cb_recv.at[pl.ds(cb0, 56), :], CB + step)
        near = cb_recv[cb0 : cb0 + 8, :]
        for y in range(1, NY):
            near = near + cb_recv[cb0 + 8 * y : cb0 + 8 * y + 8, :]
        npts = [jnp.where(row8 == 0, near[k : k + 1], near[4 + k : 5 + k]) for k in range(3)]
        _, nforces = membrane(npts)
        for s in range(2):
            for k in range(3):
                near_src[s * 8 + k : s * 8 + k + 1, :PT] = near[4 * s + k : 4 * s + k + 1]
                near_src[s * 8 + 3 + k : s * 8 + 4 + k, :PT] = nforces[k][s : s + 1] * VISCOSITY
                near_rows[4 * s + k : 4 * s + k + 1, :PT] = jnp.sum(
                    jnp.where(row8 == t_of[s], pts[k], 0.0), axis=0, keepdims=True
                )
        near_cols[...] = near_rows[...].T

        def near_block(i, c):
            at = pl.multiple_of(i * 32, 32)
            cols = near_cols[pl.ds(at, 32), :]
            for s in range(2):
                t = [
                    jnp.broadcast_to(cols[:, 4 * s + k : 4 * s + k + 1], (32, 128))
                    for k in range(3)
                ]
                acc = tuple(jnp.zeros((32, 128), F32) for k in range(3))
                for q in range(PP // 128):
                    src = near_src[s * 8 : s * 8 + 8, q * 128 : q * 128 + 128]
                    acc = pair(t, [row_of(src, j, 32) for j in range(6)], acc)
                for k in range(3):
                    near_acc[pl.ds((3 * s + k) * PP + at, 32), :] = acc[k]
            return c

        lax.fori_loop(0, PT // 32, near_block, 0)
        nv = []
        for i in range(6):
            summed = jnp.sum(near_acc[i * PP : (i + 1) * PP, :].T, axis=0, keepdims=True)
            nv.append(summed[:, :PT])

        arrived(gp_buf.at[pl.ds(gp0, 184), :], GP + step)
        sources(src_grp, gp_buf, gp0, NG, 8, grp, GROUP_RADIUS, center)
        far(src_grp, NG, False)
        ones = jnp.ones((16, 128), BF)
        checks = []
        for k in range(3):
            ah, al = halves(acc_ref[k * Q : (k + 1) * Q, :])
            dims = (((1,), (1,)), ((), ()))
            checks.append(
                (
                    lax.dot_general(ones, ah, dims, preferred_element_type=F32)
                    + lax.dot_general(ones, al, dims, preferred_element_type=F32)
                )[:8]
            )
        surface = mm(jnp.concatenate(checks, axis=0), dn_hi, dn_lo)

        for k in range(3):
            v = surface[8 * k : 8 * k + 8]
            for s in range(2):
                v = v + jnp.where((row8 == t_of[s]) & used[s], nv[3 * s + k], 0.0)
            pts[k] = pts[k] + TIME_STEP * v
            if step == STEPS - 1:
                vel_ref[8 * k : 8 * k + 8, :] = v
                new_ref[8 * k : 8 * k + 8, :] = pts[k]

    for step in range(STEPS):
        left(eq_buf.at[pl.ds(0, 248), :], EQ + step)
        left(gp_buf.at[pl.ds(0, 184), :], GP + step)
        left(ca_buf.at[pl.ds(0, 48), :], CA + step)
        left(cb_send.at[pl.ds(0, 56), :], CB + step)
    left(rq_send.at[pl.ds(0, 56), :], RQ)


def body(
    positions,
    rest_shape,
    stiffness,
    up_map,
    down_map,
    m2m,
    box_template,
    near_target,
    near_owner,
    near_cell,
    near_count,
):
    def spread(a):
        gap = jnp.zeros((a.shape[0], 8), F32)
        rest = a[:, 128:]
        return jnp.concatenate([a[:, :128]] + [rest, gap] * 4, axis=1)

    padded = jnp.pad(positions, ((0, 0), (0, 4), (0, 0))).reshape(24, PT)
    m2 = spread(spread(m2m).T).T
    vmem = pl.BlockSpec(memory_space=pltpu.VMEM)
    smem = pl.BlockSpec(memory_space=pltpu.SMEM)
    shape = jax.ShapeDtypeStruct((24, PT), F32)
    new, vel = pl.pallas_call(
        kernel,
        out_shape=(shape, shape),
        in_specs=[smem] * 4 + [vmem] * 8,
        out_specs=(vmem, vmem),
        scratch_shapes=[
            pltpu.VMEM((PT, PT), BF),
            pltpu.VMEM((PT, PT), BF),
            pltpu.VMEM((PT, 256), BF),
            pltpu.VMEM((PT, 256), BF),
            pltpu.VMEM((256, 256), BF),
            pltpu.VMEM((256, 256), BF),
            pltpu.VMEM((Q, PT), BF),
            pltpu.VMEM((Q, PT), BF),
            pltpu.VMEM((3 * Q, 128), F32),
            pltpu.VMEM((3 * Q, 128), F32),
            pltpu.VMEM((STEPS * 256, 128), F32),
            pltpu.VMEM((STEPS * 192, 128), F32),
            pltpu.VMEM((STEPS * 64, PT), F32),
            pltpu.VMEM((STEPS * 64, PT), F32),
            pltpu.VMEM((STEPS * 64, PT), F32),
            pltpu.VMEM((64, 128), jnp.int32),
            pltpu.VMEM((64, 128), jnp.int32),
            pltpu.VMEM((6 * 40, 128), F32),
            pltpu.VMEM((6 * 32, 128), F32),
            pltpu.VMEM((16, PP), F32),
            pltpu.VMEM((8, PP), F32),
            pltpu.VMEM((PP, 8), F32),
            pltpu.VMEM((6 * PP, 128), F32),
            pltpu.SemaphoreType.DMA((9,)),
            pltpu.SemaphoreType.DMA((9,)),
        ],
        compiler_params=pltpu.CompilerParams(
            collective_id=0, has_side_effects=True, vmem_limit_bytes=40 * 1024 * 1024
        ),
    )(
        near_target,
        near_owner,
        near_cell,
        near_count,
        padded,
        rest_shape,
        stiffness,
        spread(up_map),
        m2,
        down_map,
        box_template.T,
        spread(box_template),
    )
    return (
        new.reshape(3, 8, PT)[:, :4],
        vel.reshape(3, 8, PT)[:, :4],
    )


def solution(mesh):
    return jax.shard_map(
        body,
        mesh=mesh,
        in_specs=(
            P(None, ("grp", "dev"), None),
            P(),
            P(),
            P(),
            P(),
            P(),
            P(),
            P(("grp", "dev"), None),
            P(("grp", "dev"), None),
            P(("grp", "dev"), None),
            P(("grp", "dev")),
        ),
        out_specs=(P(None, ("grp", "dev"), None), P(None, ("grp", "dev"), None)),
        check_vma=False,
    )
```

time: 271 us -> 69.1 us (0.25)
  the two profiles are of different devices: /device:TPU:8 before, /device:TPU:1 now
where the time goes in v1:
time: 69.1 us; the launch traced here: 68.3 us
  Pallas kernels  61.4 us (89%)
  local copies, waits for them, and re-layouts  5.37 us (8%)
  between operations  1.51 us (2%)
    pallas_call x1, Pallas kernels, body(): pl.pallas_call(kernel, out_shape=(shape, shape), in_specs=[smem] * 4 + [v...  61.4 us
    unnamed x25, local copies, waits for them, and re-layouts  2.11 us

profile of v1, /device:TPU:1, one launch (start us, length us, event | category | flops | bytes accessed | tf_op | source)
XLA Modules:
  0.0 68.3 jit_solution(2920388103545445727)
XLA Ops:
  1.3 0.8 %pad_bitcast_fusion.pos_ref = f32[24,544]{1,0:T(8,128)S(1)} fusion(f32[3,4,544]{2,1,0:T(4,128)} %param.11), kind=kLoop, calls=%fused_computation | loop fusion | bytes 78336 | tf_op jit(solution)/shard_map/reshape | solution.py:416
  2.0 1.2 %copy.14 = f32[544,152]{1,0:T(8,128)S(1)} copy(f32[544,152]{0,1:T(8,128)} %param.14) | data formatting | bytes 661504 | tf_op args[3]
  3.3 0.0 copy-start.6
  3.3 0.0 slice-start
  3.3 0.0 copy-start.1
  3.3 0.9 %concatenate.14.up_ref = f32[544,256]{1,0:T(8,128)S(1)} concatenate(f32[544,152]{1,0:T(8,128)S(1)} %copy.14, f32[544,8]{1,0:T(8,128)S(1)} %broadcast_in_dim.9, f32[544,24]{1,0:T(8,128)S(1)} %slice.32, f32[544,8]{1,0:T(8,128)S(1)} %broadcast_in_dim.9, f32[544,24]{1,0:T(8,128)S(1)} %slice.32, f32[544,8]{1,0:T(8,128)S(1)} %broadcast_in_dim.9, f32[544,24]{1,0:T(8,128)S(1)} %slice.32, ...), dimensions={1} | concatenate | bytes 1114112 | tf_op jit(solution)/shard_map/concatenate | solution.py:414
  4.2 0.0 copy-start.7
  4.2 0.0 slice-start.1
  4.2 0.0 copy-start
  4.3 0.0 copy-start.2
  4.3 0.0 copy-start.3
  4.3 0.0 copy-start.4
  4.3 0.0 copy-start.5
  4.3 0.0 copy-done.6
  4.3 0.0 slice-done
  4.3 0.2 concatenate.15
  4.7 0.2 copy-done.7
  4.9 0.1 copy.15
  5.0 0.0 slice-done.1
  5.0 0.1 concatenate.17.rows_ref
  5.1 0.0 copy-done.1
  5.1 0.5 copy-done
  5.6 0.0 copy-done.2
  5.6 0.0 copy-done.3
  5.6 0.0 copy-done.4
  5.6 0.0 copy-done.5
  5.6 61.4 %shard_map.122 = (f32[24,544]{1,0:T(8,128)S(1)}, f32[24,544]{1,0:T(8,128)S(1)}) custom-call(s32[1,2]{1,0:T(1,128)S(1)} %copy-done.3, s32[1,2]{1,0:T(1,128)S(1)} %copy-done.4, s32[1,2]{1,0:T(1,128)S(1)} %copy-done.5, s32[1]{0:T(128)S(6)} %copy.23.near_count, f32[24,544]{1,0:T(8,128)S(1)} %pad_bitcast_fusion.pos_ref, f32[3,544]{1,0:T(4,128)S(1)} %copy-done.2, ...), custom_call_target="tpu_custom_call" | custom-call | tf_op jit(solution)/shard_map/pallas_call | solution.py:421
  67.1 0.6 slice.34
  67.7 0.6 slice.35
  (12 shorter events, 0.1 us)
Async XLA Ops:
  3.3 1.0 %copy-start.6 = (f32[152,152]{1,0:T(8,128)S(1)}, f32[152,152]{1,0:T(8,128)}, u32[]{:S(2)}) copy-start(f32[152,152]{1,0:T(8,128)} %param.16) | copy-start | bytes 277252
  3.3 1.0 %slice-start = ((f32[152,152]{1,0:T(8,128)}), f32[152,24]{1,0:T(8,128)S(1)}, s32[]{:S(2)}) async-start(f32[152,152]{1,0:T(8,128)} %param.16), calls=%async_computation | async-start | bytes 155648 | tf_op jit(solution)/shard_map/slice | solution.py:413
  3.3 1.8 %copy-start.1 = (f32[152,544]{1,0:T(8,128)S(1)}, f32[152,544]{1,0:T(8,128)}, u32[]{:S(2)}) copy-start(f32[152,544]{1,0:T(8,128)} %down_ref.1) | copy-start | bytes 992260
  4.2 0.7 %copy-start.7 = (f32[3,152]{1,0:T(4,128)S(1)}, f32[3,152]{1,0:T(4,128)}, u32[]{:S(2)}) copy-start(f32[3,152]{1,0:T(4,128)} %param.17) | copy-start | bytes 5476
  4.2 0.8 %slice-start.1 = ((f32[3,152]{1,0:T(4,128)}), f32[3,24]{1,0:T(4,128)S(1)}, s32[]{:S(2)}) async-start(f32[3,152]{1,0:T(4,128)} %param.17), calls=%async_computation.1 | async-start | bytes 4096 | tf_op jit(solution)/shard_map/slice | solution.py:413
  4.2 1.4 %copy-start = (f32[544,544]{1,0:T(8,128)S(1)}, f32[544,544]{1,0:T(8,128)}, u32[]{:S(2)}) copy-start(f32[544,544]{1,0:T(8,128)} %stiff_ref.1) | copy-start | bytes 3551236
  4.3 1.4 %copy-start.2 = (f32[3,544]{1,0:T(4,128)S(1)}, f32[3,544]{1,0:T(4,128)}, u32[]{:S(2)}) copy-start(f32[3,544]{1,0:T(4,128)} %rest_ref.1) | copy-start | bytes 19588
  4.3 1.4 %copy-start.3 = (s32[1,2]{1,0:T(1,128)S(1)}, s32[1,2]{1,0:T(1,128)}, u32[]{:S(2)}) copy-start(s32[1,2]{1,0:T(1,128)} %near_target.1) | copy-start | bytes 28
  4.3 1.4 %copy-start.4 = (s32[1,2]{1,0:T(1,128)S(1)}, s32[1,2]{1,0:T(1,128)}, u32[]{:S(2)}) copy-start(s32[1,2]{1,0:T(1,128)} %near_owner.1) | copy-start | bytes 28
  4.3 1.4 %copy-start.5 = (s32[1,2]{1,0:T(1,128)S(1)}, s32[1,2]{1,0:T(1,128)}, u32[]{:S(2)}) copy-start(s32[1,2]{1,0:T(1,128)} %near_cell.1) | copy-start | bytes 28

commit v2 on v1

v2 whole, which is shorter than its diff:
```python
import functools

import jax
import jax.numpy as jnp
from jax import lax
from jax.experimental import pallas as pl
from jax.experimental.pallas import tpu as pltpu
from jax.sharding import PartitionSpec as P

STEPS = 2
EPS = 0.25
VISCOSITY = 0.039788735772973836
TIME_STEP = 0.1
SKALAK_HARDEN = 2.0
CHECK_RADIUS = 1.0
DEVICE_RADIUS = 1.5
GROUP_RADIUS = 6.0

NG = 24
ND = 32
NX = 4
NY = 8
PT = 544
PP = 640
Q = 152
F32 = jnp.float32
BF = jnp.bfloat16
MESH = pl.DeviceIdType.MESH

QP = 160
DEV_OFF = sorted(
    [(x, y) for x in range(NX) for y in range(NY) if (x, y) != (0, 0)],
    key=lambda o: (min(o[0], NX - o[0]) + min(o[1], NY - o[1]), o),
)
GRP_OFF = sorted(range(1, NG), key=lambda o: (min(o, NG - o), o))
DEV_SLOT = {o: i for i, o in enumerate(DEV_OFF)}
GRP_SLOT = {o: i for i, o in enumerate(GRP_OFF)}
EQ, GP, CA, CB, RQ = 0, 8, 14, 16, 18


def halves(w):
    hi = w.astype(BF)
    return hi, (w - hi.astype(F32)).astype(BF)


def dot(a, b):
    return jnp.dot(a, b, preferred_element_type=F32)


def dot_t(a, b):
    return lax.dot_general(a, b, (((1,), (1,)), ((), ())), preferred_element_type=F32)


def mm(a, hi, lo):
    ah, al = halves(a)
    return dot(ah, hi[...]) + dot(al, hi[...]) + dot(ah, lo[...])


def pair(t, s, acc):
    tx, ty, tz = t
    sx, sy, sz, fx, fy, fz = s
    dx, dy, dz = tx - sx, ty - sy, tz - sz
    rs = lax.rsqrt(dx * dx + dy * dy + (dz * dz + EPS))
    b = rs * rs * rs
    direct = rs + EPS * b
    proj = (dx * fx + dy * fy + dz * fz) * b
    return (
        acc[0] + (direct * fx + proj * dx),
        acc[1] + (direct * fy + proj * dy),
        acc[2] + (direct * fz + proj * dz),
    )


def row_of(tile, j, rows):
    return jnp.broadcast_to(tile[j : j + 1, :], (rows, 128))


def kernel(
    *refs
):
    inputs, (new_ref, vel_ref), local = refs[:11], refs[11:13], refs[13:24]
    (
        st_hi,
        st_lo,
        up_hi,
        up_lo,
        mm_hi,
        mm_lo,
        dn_hi,
        dn_lo,
        box_rows,
        targets,
        acc_ref,
        eq_msg,
        gp_msg,
        eq_buf,
        gp_buf,
        ca_buf,
        cb_send,
        cb_recv,
        rq_send,
        rq_recv,
        src_ref,
        near_src,
        near_rows,
        near_cols,
        near_acc,
        send_sem,
        recv_sem,
        load_sem,
    ) = refs[24:]
    loads = [
        pltpu.make_async_copy(a, b, load_sem.at[i])
        for i, (a, b) in enumerate(zip(inputs, local))
    ]
    for load in loads:
        load.start()
    (
        near_target,
        near_owner,
        near_cell,
        near_count,
        pos_ref,
        rest_ref,
        stiff_ref,
        up_ref,
        m2m_ref,
        down_ref,
        box_ref,
    ) = local
    me = lax.axis_index("dev")
    grp = lax.axis_index("grp")
    mx = me // NY
    my = me % NY

    barrier = pltpu.get_barrier_semaphore()

    def greet(axis, own, count):
        def one(i, c):
            pl.semaphore_signal(
                barrier, inc=1, device_id={axis: lax.rem(own + i, count)}, device_id_type=MESH
            )
            return c

        lax.fori_loop(1, count, one, 0)

    greet("dev", me, ND)
    greet("grp", grp, NG)

    def push(src, dst, sem, device, arrival=None):
        pltpu.make_async_remote_copy(
            src_ref=src,
            dst_ref=dst,
            send_sem=send_sem.at[sem],
            recv_sem=recv_sem.at[sem if arrival is None else arrival],
            device_id=device,
            device_id_type=MESH,
        ).start()

    def arrived(ref, sem):
        pltpu.make_async_copy(ref, ref, recv_sem.at[sem]).wait()

    def left(ref, sem):
        pltpu.make_async_copy(ref, ref, send_sem.at[sem]).wait()

    def send_boxes(step):
        for x, y in reversed(DEV_OFF):
            slot = DEV_SLOT[((NX - x) % NX, (NY - y) % NY)]
            peer = lax.rem(mx + x, NX) * NY + lax.rem(my + y, NY)
            push(
                eq_msg.at[step],
                eq_buf.at[step * 32 + slot],
                EQ + 4 * step,
                {"dev": peer},
                EQ + 4 * step + slot // 8,
            )

    def send_groups(step):
        for o in reversed(GRP_OFF):
            slot = GRP_SLOT[NG - o]
            push(
                gp_msg.at[step],
                gp_buf.at[step * 24 + slot],
                GP + 3 * step,
                {"grp": lax.rem(grp + o, NG)},
                GP + 3 * step + slot // 8,
            )

    for load in loads:
        load.wait()

    def spread(a, axis):
        shape = list(a.shape)
        shape[axis] = 8
        gap = jnp.zeros(shape, F32)
        main, rest = (a[:, :128], a[:, 128:]) if axis else (a[:128], a[128:])
        return jnp.concatenate([main] + [rest, gap] * 4, axis=axis)

    st_hi[...], st_lo[...] = halves(stiff_ref[...])
    up_hi[...], up_lo[...] = halves(spread(up_ref[...], 0))
    mm_hi[0:Q, :], mm_lo[0:Q, :] = halves(spread(m2m_ref[...], 1))
    mm_hi[Q:, :] = jnp.zeros((8, 256), BF)
    mm_lo[Q:, :] = jnp.zeros((8, 256), BF)
    dn_hi[...], dn_lo[...] = halves(down_ref[...])
    box_rows[...] = jnp.zeros_like(box_rows)
    box_rows[0:3, 0:Q] = box_ref[...]
    cols = box_rows[...].T
    for k in range(3):
        targets[k * QP : (k + 1) * QP, :] = jnp.broadcast_to(
            CHECK_RADIUS * cols[:QP, k : k + 1], (QP, 128)
        )
    box_rows[0:3, :] = spread(box_ref[...], 1)
    for step in range(STEPS):
        eq_buf[step * 32 + 31] = jnp.zeros((4, 128), F32)
        gp_buf[step * 24 + 23] = jnp.zeros((4, 128), F32)
    near_src[...] = jnp.zeros_like(near_src)
    near_rows[...] = jnp.zeros_like(near_rows)
    near_acc[...] = jnp.zeros_like(near_acc)

    sub = lax.broadcasted_iota(jnp.int32, (8, 128), 0)
    lane = lax.broadcasted_iota(jnp.int32, (8, 128), 1)
    row8 = lax.broadcasted_iota(jnp.int32, (8, PT), 0)
    count = near_count[0]
    t_of = [near_target[0, s] for s in range(2)]
    used = [s < count for s in range(2)]

    want, from_y = [], []
    for s in range(2):
        owner = near_owner[0, s]
        want.append((owner // NY) * 16 + near_cell[0, s])
        from_y.append(jnp.where(used[s], owner % NY, -1))
    kk = sub % 4
    slot_want = jnp.where(sub < 4, want[0], want[1]) + 4 * kk
    slot_y = jnp.where(sub < 4, from_y[0], from_y[1])
    for y in range(NY):
        rq_send[y * 8 : (y + 1) * 8, :] = jnp.where((slot_y == y) & (kk < 3), slot_want, -1)

    def membrane(pts):
        cents, strain = [], []
        for k in range(3):
            c = jnp.sum(pts[k], axis=1, keepdims=True) * (1.0 / PT)
            cents.append(c)
            strain.append(pts[k] - c - rest_ref[k : k + 1, :])
        flat = jnp.concatenate(strain, axis=0)
        hi = flat.astype(BF).astype(F32)
        both = jnp.concatenate([hi, flat - hi], axis=0).astype(BF)
        first = dot(both, st_hi[...])
        linear = first[:24] + first[24:] + dot(both[:32], st_lo[...])[:24]
        lin = [linear[8 * k : 8 * k + 8] for k in range(3)]
        stretch = lin[0] * lin[0] + lin[1] * lin[1] + lin[2] * lin[2]
        harden = 1.0 + SKALAK_HARDEN * stretch / (1.0 + stretch)
        return cents, [-l * harden for l in lin]

    def own_cells(pts):
        return jnp.concatenate([p[:4] for p in pts] + [jnp.zeros((4, PT), F32)], axis=0)

    def message(e, center):
        rest = jnp.where(lane == 96, center[0], jnp.where(lane == 97, center[1], center[2]))
        for k in range(3):
            rest = jnp.where(lane // 32 == k, e[k : k + 1, 128:], rest)
        return jnp.where(sub < 3, e[:, :128], rest)[:4]

    def sources(buf, base, at, radius, center):
        rest = buf[pl.ds(base, 8), 3, :]
        turned = [rest] + [pltpu.roll(rest, 32 * m, 1) for m in range(1, 4)]
        place = (lane // 32) == (sub % 4)
        for k in range(3):
            f = buf[pl.ds(base, 8), k, :]
            r = turned[(0 - k) % 4]
            for j in range(1, 4):
                r = jnp.where(sub % 4 == j, turned[(j - k) % 4], r)
            r = jnp.where(place, r, 0.0) * VISCOSITY
            at_f = at + (3 + k) * 16
            src_ref[at_f : at_f + 8, :] = f * VISCOSITY
            src_ref[at_f + 8 : at_f + 9, :] = jnp.sum(r[:4], axis=0, keepdims=True)
            src_ref[at_f + 9 : at_f + 10, :] = jnp.sum(r[4:], axis=0, keepdims=True)
            c = jnp.broadcast_to(rest[:, 96 + k : 97 + k] - center[k], (8, 128))
            pc = jnp.where(place, c, 0.0)
            at_c = at + k * 16
            src_ref[at_c : at_c + 8, :] = c + radius * box_rows[k : k + 1, :128]
            more = radius * box_rows[k : k + 1, 128:]
            src_ref[at_c + 8 : at_c + 9, :] = jnp.sum(pc[:4], axis=0, keepdims=True) + more
            src_ref[at_c + 9 : at_c + 10, :] = jnp.sum(pc[4:], axis=0, keepdims=True) + more

    def far(at):
        def one(i, c):
            rows = [pl.ds(pl.multiple_of(k * QP + i * 16, 16), 16) for k in range(3)]
            t = [targets[r, :] for r in rows]
            acc = tuple(acc_ref[r, :] for r in rows)
            tiles = [src_ref[at + 16 * k : at + 16 * k + 16, :] for k in range(6)]
            for j in range(10):
                acc = pair(t, [row_of(x, j, 16) for x in tiles], acc)
            for r, a in zip(rows, acc):
                acc_ref[r, :] = a
            return c

        lax.fori_loop(0, QP // 16, one, 0)

    pts = [
        jnp.concatenate([pos_ref[k], jnp.zeros((4, PT), F32)], axis=0) for k in range(3)
    ]
    for step in range(STEPS):
        ca0, cb0 = step * 64, step * 64
        cells = ca_buf.at[pl.ds(pl.multiple_of(ca0 + mx * 16, 8), 16), :]

        def send_cells():
            for i in (2, 1, 3):
                push(cells, cells, CA + step, {"dev": lax.rem(mx + i, NX) * NY + my})

        ca_buf[pl.ds(pl.multiple_of(ca0 + mx * 16, 8), 16), :] = own_cells(pts)
        if step > 0:
            send_cells()
        acc_ref[...] = jnp.zeros_like(acc_ref)
        cents, forces = membrane(pts)
        center = [jnp.sum(c[:4], axis=0, keepdims=True) * 0.25 for c in cents]
        total = [jnp.sum(f[:4], axis=0, keepdims=True) for f in forces]
        m3 = row8 % 3
        fs = jnp.where(m3 == 0, total[0], jnp.where(m3 == 1, total[1], total[2]))
        fh, fl = halves(fs)
        msg = message(dot_t(fh, up_hi[...]) + dot_t(fl, up_hi[...]) + dot_t(fh, up_lo[...]), center)
        eq_msg[step] = msg

        if step == 0:
            pl.semaphore_wait(barrier, ND - 1 + NG - 1)
        send_boxes(step)
        mine = pl.ds(pl.multiple_of(my * 8, 8), 8)
        if step == 0:
            send_cells()
            for i in (4, 3, 5, 2, 6, 1, 7):
                y = lax.rem(my + i, NY)
                push(
                    rq_send.at[pl.ds(pl.multiple_of(y * 8, 8), 8), :],
                    rq_recv.at[mine, :],
                    RQ,
                    {"dev": mx * NY + y},
                )
            rq_recv[mine, :] = rq_send[mine, :]

        def box_class(c):
            sources(eq_buf, step * 32 + 8 * c, c * 96, DEVICE_RADIUS, center)

        def wait_boxes(c):
            n = 7 if c == 3 else 8
            arrived(eq_buf.at[pl.ds(step * 32 + 8 * c, n)], EQ + 4 * step + c)

        def wait_groups(c):
            n = 7 if c == 2 else 8
            arrived(gp_buf.at[pl.ds(step * 24 + 8 * c, n)], GP + 3 * step + c)

        def group_class(c):
            wait_groups(c)
            sources(gp_buf, step * 24 + 8 * c, (4 + c) * 96, GROUP_RADIUS, center)
            far((4 + c) * 96)

        wait_boxes(0)
        box_class(0)
        far(0)
        if step == 0:
            arrived(rq_recv.at[pl.ds(0, 56), :], RQ)
        arrived(ca_buf.at[pl.ds(ca0, 48), :], CA + step)

        pick = rq_recv[:, :64] == lax.broadcasted_iota(jnp.int32, (64, 64), 1)
        pick = jnp.where(pick, 1.0, 0.0).astype(BF)
        cells = ca_buf[ca0 : ca0 + 64, :]
        c1 = cells.astype(BF)
        cells = cells - c1.astype(F32)
        c2 = cells.astype(BF)
        c3 = (cells - c2.astype(F32)).astype(BF)
        cb_send[cb0 : cb0 + 64, :] = (dot(pick, c1) + dot(pick, c2)) + dot(pick, c3)
        own_b = pl.ds(pl.multiple_of(cb0 + my * 8, 8), 8)
        for i in (4, 3, 5, 2, 6, 1, 7):
            y = lax.rem(my + i, NY)
            push(
                cb_send.at[pl.ds(pl.multiple_of(cb0 + y * 8, 8), 8), :],
                cb_recv.at[own_b, :],
                CB + step,
                {"dev": mx * NY + y},
            )
        cb_recv[own_b, :] = cb_send[own_b, :]

        for c in (1, 2):
            wait_boxes(c)
            box_class(c)
            far(c * 96)
        wait_boxes(3)
        parts = [eq_buf[step * 32 + i] for i in range(ND - 1)] + [msg]
        while len(parts) > 1:
            parts = [a + b for a, b in zip(parts[::2], parts[1::2])]
        tile = parts[0]
        last = tile[3:4, :]
        main = jnp.concatenate([tile, jnp.zeros((4, 128), F32)], axis=0)
        tail = jnp.broadcast_to(last, (8, 128))
        rest = tail
        for k in range(1, 3):
            rest = jnp.where(sub == k, pltpu.roll(tail, 128 - 32 * k, 1), rest)
        rest = rest[:, :32]
        middle = [last[:, 96 + k : 97 + k] * (1.0 / ND) for k in range(3)]
        group = mm(main, mm_hi[:128], mm_lo[:128]) + mm(rest, mm_hi[128:], mm_lo[128:])
        gp_msg[step] = message(group, middle)
        send_groups(step)

        box_class(3)
        far(3 * 96)

        arrived(cb_recv.at[pl.ds(cb0, 56), :], CB + step)
        near = cb_recv[cb0 : cb0 + 8, :]
        for y in range(1, NY):
            near = near + cb_recv[cb0 + 8 * y : cb0 + 8 * y + 8, :]
        npts = [jnp.where(row8 == 0, near[k : k + 1], near[4 + k : 5 + k]) for k in range(3)]
        _, nforces = membrane(npts)
        for s in range(2):
            for k in range(3):
                near_src[s * 8 + k : s * 8 + k + 1, :PT] = near[4 * s + k : 4 * s + k + 1]
                near_src[s * 8 + 3 + k : s * 8 + 4 + k, :PT] = nforces[k][s : s + 1] * VISCOSITY
                near_rows[4 * s + k : 4 * s + k + 1, :PT] = jnp.sum(
                    jnp.where(row8 == t_of[s], pts[k], 0.0), axis=0, keepdims=True
                )
        near_cols[...] = near_rows[...].T

        def near_block(i, c):
            at = pl.multiple_of(i * 32, 32)
            cols = near_cols[pl.ds(at, 32), :]
            for s in range(2):
                t = [
                    jnp.broadcast_to(cols[:, 4 * s + k : 4 * s + k + 1], (32, 128))
                    for k in range(3)
                ]
                acc = tuple(jnp.zeros((32, 128), F32) for k in range(3))
                for q in range(PP // 128):
                    src = near_src[s * 8 : s * 8 + 8, q * 128 : q * 128 + 128]
                    acc = pair(t, [row_of(src, j, 32) for j in range(6)], acc)
                for k in range(3):
                    near_acc[pl.ds((3 * s + k) * PP + at, 32), :] = acc[k]
            return c

        lax.fori_loop(0, PT // 32, near_block, 0)
        nv = []
        for i in range(6):
            summed = jnp.sum(near_acc[i * PP : (i + 1) * PP, :].T, axis=0, keepdims=True)
            nv.append(summed[:, :PT])

        for c in range(3):
            group_class(c)
        ones = jnp.ones((16, 128), BF)
        checks = []
        for k in range(3):
            ah, al = halves(acc_ref[k * QP : k * QP + Q, :])
            dims = (((1,), (1,)), ((), ()))
            checks.append(
                (
                    lax.dot_general(ones, ah, dims, preferred_element_type=F32)
                    + lax.dot_general(ones, al, dims, preferred_element_type=F32)
                )[:8]
            )
        surface = mm(jnp.concatenate(checks, axis=0), dn_hi, dn_lo)

        for k in range(3):
            v = surface[8 * k : 8 * k + 8]
            for s in range(2):
                v = v + jnp.where((row8 == t_of[s]) & used[s], nv[3 * s + k], 0.0)
            pts[k] = pts[k] + TIME_STEP * v
            if step == STEPS - 1:
                vel_ref[k] = v[:4]
                new_ref[k] = pts[k][:4]

    for step in range(STEPS):
        left(eq_buf.at[pl.ds(0, 31)], EQ + 4 * step)
        left(gp_buf.at[pl.ds(0, 23)], GP + 3 * step)
        left(ca_buf.at[pl.ds(0, 48), :], CA + step)
        left(cb_send.at[pl.ds(0, 56), :], CB + step)
    left(rq_send.at[pl.ds(0, 56), :], RQ)


def body(
    positions,
    rest_shape,
    stiffness,
    up_map,
    down_map,
    m2m,
    box_template,
    near_target,
    near_owner,
    near_cell,
    near_count,
):
    vmem = pl.BlockSpec(memory_space=pltpu.VMEM)
    hbm = pl.BlockSpec(memory_space=pltpu.HBM)
    arrays = (
        near_target,
        near_owner,
        near_cell,
        near_count,
        positions,
        rest_shape,
        stiffness,
        up_map.T,
        m2m,
        down_map,
        box_template,
    )
    shape = jax.ShapeDtypeStruct(positions.shape, F32)
    return pl.pallas_call(
        kernel,
        out_shape=(shape, shape),
        in_specs=[hbm] * 11,
        out_specs=(vmem, vmem),
        scratch_shapes=[pltpu.SMEM(a.shape, a.dtype) for a in arrays[:4]]
        + [pltpu.VMEM(a.shape, a.dtype) for a in arrays[4:]]
        + [
            pltpu.VMEM((PT, PT), BF),
            pltpu.VMEM((PT, PT), BF),
            pltpu.VMEM((256, PT), BF),
            pltpu.VMEM((256, PT), BF),
            pltpu.VMEM((QP, 256), BF),
            pltpu.VMEM((QP, 256), BF),
            pltpu.VMEM((Q, PT), BF),
            pltpu.VMEM((Q, PT), BF),
            pltpu.VMEM((8, 256), F32),
            pltpu.VMEM((3 * QP, 128), F32),
            pltpu.VMEM((3 * QP, 128), F32),
            pltpu.VMEM((STEPS, 4, 128), F32),
            pltpu.VMEM((STEPS, 4, 128), F32),
            pltpu.VMEM((STEPS * 32, 4, 128), F32),
            pltpu.VMEM((STEPS * 24, 4, 128), F32),
            pltpu.VMEM((STEPS * 64, PT), F32),
            pltpu.VMEM((STEPS * 64, PT), F32),
            pltpu.VMEM((STEPS * 64, PT), F32),
            pltpu.VMEM((64, 128), jnp.int32),
            pltpu.VMEM((64, 128), jnp.int32),
            pltpu.VMEM((7 * 96, 128), F32),
            pltpu.VMEM((16, PP), F32),
            pltpu.VMEM((8, PP), F32),
            pltpu.VMEM((PP, 8), F32),
            pltpu.VMEM((6 * PP, 128), F32),
            pltpu.SemaphoreType.DMA((19,)),
            pltpu.SemaphoreType.DMA((19,)),
            pltpu.SemaphoreType.DMA((11,)),
        ],
        compiler_params=pltpu.CompilerParams(
            collective_id=0, has_side_effects=True
        ),
    )(*arrays)


def solution(mesh):
    return jax.shard_map(
        body,
        mesh=mesh,
        in_specs=(
            P(None, ("grp", "dev"), None),
            P(),
            P(),
            P(),
            P(),
            P(),
            P(),
            P(("grp", "dev"), None),
            P(("grp", "dev"), None),
            P(("grp", "dev"), None),
            P(("grp", "dev")),
        ),
        out_specs=(P(None, ("grp", "dev"), None), P(None, ("grp", "dev"), None)),
        check_vma=False,
    )
```

time: 69.1 us -> 64.8 us (0.938)
  local copies, waits for them, and re-layouts: 5.37 us -> 2.73 us
  Pallas kernels: 61.4 us -> 60.5 us
    slice x7 -> x0, local copies, waits for them, and re-layouts: 1.26 us -> none  [the longest x2 1.23 us: body(): return (new.reshape(3, 8, PT)[:, :4], vel.reshape(3, 8, PT)[:, :4])]
    concatenate x4 -> x0, local copies, waits for them, and re-layouts: 1.21 us -> none  [spread(): return jnp.concatenate([a[:, :128]] + [rest, gap] * 4, axis=1)]
    pallas_call x1, Pallas kernels: 61.4 us -> 60.5 us  [body(): pl.pallas_call(kernel, out_shape=(shape, shape), in_specs=[hbm] * 11, out...]
    reshape x1 -> x0, local copies, waits for them, and re-layouts: 0.76 us -> none  [body(): padded = jnp.pad(positions, ((0, 0), (0, 4), (0, 0))).reshape(24, PT)]
    unnamed x25 -> x2, local copies, waits for them, and re-layouts: 2.11 us -> 2.73 us
where the time goes in v2:
time: 64.8 us; the launch traced here: 64.5 us
  Pallas kernels  60.5 us (93%)
  local copies, waits for them, and re-layouts  2.73 us (4%)
  between operations  1.29 us (2%)
    pallas_call x1, Pallas kernels, body(): pl.pallas_call(kernel, out_shape=(shape, shape), in_specs=[hbm] * 11, out...  60.5 us
    unnamed x2, local copies, waits for them, and re-layouts  2.73 us

profile of v2, /device:TPU:1, one launch (start us, length us, event | category | flops | bytes accessed | tf_op | source)
XLA Modules:
  0.0 64.5 jit_solution(14144427664772588618)
XLA Ops:
  1.3 60.5 %shard_map.122 = (f32[3,4,544]{2,1,0:T(4,128)}, f32[3,4,544]{2,1,0:T(4,128)}) custom-call(s32[1,2]{1,0:T(1,128)} %refs_0_.1, s32[1,2]{1,0:T(1,128)} %refs_1_.1, s32[1,2]{1,0:T(1,128)} %refs_2_.1, s32[1]{0:T(128)S(6)} %copy.15.refs_3_, f32[3,4,544]{2,1,0:T(4,128)} %refs_4_.1, f32[3,544]{1,0:T(4,128)} %refs_5_.1, f32[544,544]{1,0:T(8,128)} %refs_6_.1, ...), custom_call_target="tpu_custom_call" | custom-call | tf_op jit(solution)/shard_map/pallas_call | solution.py:503
  61.8 1.4 %copy.16 = f32[3,4,544]{2,1,0:T(4,128)} copy(f32[3,4,544]{2,1,0:T(4,128)} %get-tuple-element.4) | data formatting | bytes 52224
  63.1 1.4 %copy.17 = f32[3,4,544]{2,1,0:T(4,128)} copy(f32[3,4,544]{2,1,0:T(4,128)} %get-tuple-element.5) | data formatting | bytes 52224

commit v3 on v2

--- a/solution.py
+++ b/solution.py
@@ -352,9 +352,6 @@
             sources(gp_buf, step * 24 + 8 * c, (4 + c) * 96, GROUP_RADIUS, center)
             far((4 + c) * 96)
 
-        wait_boxes(0)
-        box_class(0)
-        far(0)
         if step == 0:
             arrived(rq_recv.at[pl.ds(0, 56), :], RQ)
         arrived(ca_buf.at[pl.ds(ca0, 48), :], CA + step)
@@ -378,11 +375,8 @@
             )
         cb_recv[own_b, :] = cb_send[own_b, :]
 
-        for c in (1, 2):
+        for c in range(4):
             wait_boxes(c)
-            box_class(c)
-            far(c * 96)
-        wait_boxes(3)
         parts = [eq_buf[step * 32 + i] for i in range(ND - 1)] + [msg]
         while len(parts) > 1:
             parts = [a + b for a, b in zip(parts[::2], parts[1::2])]
@@ -399,8 +393,11 @@
         gp_msg[step] = message(group, middle)
         send_groups(step)
 
-        box_class(3)
-        far(3 * 96)
+        for c in range(4):
+            box_class(c)
+            far(c * 96)
+        for c in range(2):
+            group_class(c)
 
         arrived(cb_recv.at[pl.ds(cb0, 56), :], CB + step)
         near = cb_recv[cb0 : cb0 + 8, :]
@@ -439,8 +436,7 @@
             summed = jnp.sum(near_acc[i * PP : (i + 1) * PP, :].T, axis=0, keepdims=True)
             nv.append(summed[:, :PT])
 
-        for c in range(3):
-            group_class(c)
+        group_class(2)
         ones = jnp.ones((16, 128), BF)
         checks = []
         for k in range(3):
@@ -469,6 +465,11 @@
         left(ca_buf.at[pl.ds(0, 48), :], CA + step)
         left(cb_send.at[pl.ds(0, 56), :], CB + step)
     left(rq_send.at[pl.ds(0, 56), :], RQ)
+
+
+def settle(new_ref, vel_ref, new_out, vel_out):
+    new_out[...] = new_ref[...]
+    vel_out[...] = vel_ref[...]
 
 
 def body(
@@ -500,7 +501,7 @@
         box_template,
     )
     shape = jax.ShapeDtypeStruct(positions.shape, F32)
-    return pl.pallas_call(
+    ends = pl.pallas_call(
         kernel,
         out_shape=(shape, shape),
         in_specs=[hbm] * 11,
@@ -541,6 +542,7 @@
             collective_id=0, has_side_effects=True
         ),
     )(*arrays)
+    return pl.pallas_call(settle, out_shape=(shape, shape))(*ends)
 
 
 def solution(mesh):

time: 64.8 us -> 64.7 us (level)
  local copies, waits for them, and re-layouts: 2.73 us -> 0 us
  Pallas kernels: 60.5 us -> 63.2 us
    unnamed x2 -> x0, local copies, waits for them, and re-layouts: 2.73 us -> none
    pallas_call x0 -> x1, Pallas kernels: none -> 1.39 us  [body(): return pl.pallas_call(settle, out_shape=(shape, shape))(*ends)]
    pallas_call x1, Pallas kernels: 60.5 us -> 61.8 us  [body(): pl.pallas_call(kernel, out_shape=(shape, shape), in_specs=[hbm] * 11, out...]
where the time goes in v3:
time: 64.7 us; the launch traced here: 64.5 us
  Pallas kernels  63.2 us (98%)
  between operations  1.29 us (2%)
    pallas_call x1, Pallas kernels, body(): pl.pallas_call(kernel, out_shape=(shape, shape), in_specs=[hbm] * 11, out...  61.8 us
    pallas_call x1, Pallas kernels, body(): return pl.pallas_call(settle, out_shape=(shape, shape))(*ends)  1.39 us

profile of v3, /device:TPU:1, one launch (start us, length us, event | category | flops | bytes accessed | tf_op | source)
XLA Modules:
  0.0 64.5 jit_solution(2418786874999061463)
XLA Ops:
  1.3 61.8 %shard_map.122 = (f32[3,4,544]{2,1,0:T(4,128)}, f32[3,4,544]{2,1,0:T(4,128)}) custom-call(s32[1,2]{1,0:T(1,128)} %refs_0_.1, s32[1,2]{1,0:T(1,128)} %refs_1_.1, s32[1,2]{1,0:T(1,128)} %refs_2_.1, s32[1]{0:T(128)S(6)} %copy.13.refs_3_, f32[3,4,544]{2,1,0:T(4,128)} %refs_4_.1, f32[3,544]{1,0:T(4,128)} %refs_5_.1, f32[544,544]{1,0:T(8,128)} %refs_6_.1, ...), custom_call_target="tpu_custom_call" | custom-call | tf_op jit(solution)/shard_map/pallas_call | solution.py:504
  63.1 1.4 %shard_map.123 = (f32[3,4,544]{2,1,0:T(4,128)}, f32[3,4,544]{2,1,0:T(4,128)}) custom-call(f32[3,4,544]{2,1,0:T(4,128)} %get-tuple-element.4.new_ref, f32[3,4,544]{2,1,0:T(4,128)} %get-tuple-element.5.vel_ref), custom_call_target="tpu_custom_call" | custom-call | tf_op jit(solution)/shard_map/pallas_call | solution.py:545
